TPU v7x, 32 devices: a whole 2x2x4 slice. The times are simulated.
32 devices in a mesh: pool: 4 (over y, x), slab: 8 (over z, core).
Axes of the slice: x: 2, y: 2, z: 4, core: 2. Of those that a mesh axis runs over, the one named last changes fastest.
Arguments:
- wave_coeff: bfloat16 [32, 2, 96, 9216], P(('pool', 'slab')), may hold values from -6 to 6
- response_coeff: bfloat16 [32, 2, 96, 9216], P(('pool', 'slab')), may hold values from -6 to 6
- band_index: int32 [32], P(('pool', 'slab')), may hold values from 0 to 31, each once
- occupation: int32 [32], replicated, may hold values from 0 to 2
- local_kernel: float32 [96, 9216], P('slab'), may hold values from 0.5 to 4
- gradient_kernel: float32 [96, 9216], P('slab'), may hold values from 0.25 to 2.5
Outputs:
- induced_potential: float32 [96, 9216], P('slab', 'pool')
Inputs may be any that keep to these rules, and one draw needn't show every extreme that they name: `band_index`: a permutation of the 32 band numbers.
All inputs are finite; a program needn't handle non-finite values.
Results may differ from a plain program's by a relative error of at most 0.0067.
Values sent between devices are 32-bit elements; how exact they have to be, the bound alone decides.
A program may use at most 128 MiB of HBM per device.

v0:
```python
import math

import jax
import jax.numpy as jnp
from jax import lax
from jax.sharding import PartitionSpec as P

full_turn = 2.0 * math.pi


def extended_2(array, sides, width):
    for axis, dim in sides:
        size, length = (lax.axis_size(axis), array.shape[dim])
        up = [(i, (i + 1) % size) for i in range(size)]
        down = [(j, i) for i, j in up]
        last = lax.slice_in_dim(array, length - width, length, axis=dim)
        leading = lax.slice_in_dim(array, 0, width, axis=dim)
        before = lax.ppermute(last, axis, up)
        after = lax.ppermute(leading, axis, down)
        array = jnp.concatenate([before, array, after], axis=dim)
    return array


def stacked_table(length, sign, dtype):
    indices = jnp.arange(length, dtype=jnp.int32)
    product = indices[:, None] * indices[None, :] % length
    angles = product.astype(jnp.float32) * (full_turn / length)
    factor = 1.0 / math.sqrt(length)
    cosine = jnp.cos(angles) * factor
    sine_part = jnp.sin(angles) * factor
    upper_half = jnp.stack([cosine, -sign * sine_part], axis=1)
    lower_half = jnp.stack([sign * sine_part, cosine], axis=1)
    return jnp.stack([upper_half, lower_half], axis=0).astype(dtype)


def signed_freq(length, first_wave, amount):
    waves = first_wave + jnp.arange(amount, dtype=jnp.int32)
    return jnp.where(2 * waves >= length, waves - length, waves).astype(jnp.float32)


def coulomb_kernel(length, starts, counts):
    first_freq = signed_freq(length, starts[0], counts[0])[:, None, None]
    second_freq = signed_freq(length, starts[1], counts[1])[None, :, None]
    third_freq = signed_freq(length, starts[2], counts[2])[None, None, :]
    squared = (full_turn / length) ** 2 * (
        first_freq * first_freq + second_freq * second_freq + third_freq * third_freq
    )
    nonzero = jnp.where(squared > 0, squared, 1.0)
    return jnp.where(squared > 0, full_turn / nonzero, 0.0)


def exact_pass(spec, tables, values):
    return jnp.einsum(
        spec, tables, values, precision=lax.Precision.HIGHEST, preferred_element_type=jnp.float32
    )


def half_pass(spec, tables, values):
    return jnp.einsum(spec, tables, values, preferred_element_type=jnp.float32)


def band_weights(band_index, occupation):
    numbers = jnp.arange(occupation.shape[0], dtype=jnp.int32)
    matches = band_index[:, None] == numbers[None, :]
    return jnp.sum(jnp.where(matches, occupation[None, :], 0), axis=1).astype(jnp.float32)


def weighted_intersection(wave_space, response_space, weights, factor):
    intersection = wave_space[:, 0] * response_space[:, 0] + wave_space[:, 1] * response_space[:, 1]
    return jnp.sum(weights[:, None, None, None] * intersection, axis=0) * factor


def wrapped_window(block, first_row, width):
    extended = jnp.concatenate([block[:, -2:], block, block[:, :2]], axis=1)
    return lax.dynamic_slice_in_dim(extended, first_row, width + 4, 1)


def flux_divergence(padded, coefficient):
    interior = padded[2:-2, 2:-2]
    depth_flux = coefficient[1:-1, 2:-2] * ((padded[2:, 2:-2] - padded[:-2, 2:-2]) * 0.5)
    depth_div = (depth_flux[2:] - depth_flux[:-2]) * 0.5
    across_flux = coefficient[2:-2, 1:-1] * ((padded[2:-2, 2:] - padded[2:-2, :-2]) * 0.5)
    across_div = (across_flux[:, 2:] - across_flux[:, :-2]) * 0.5
    along_flux = coefficient[2:-2, 2:-2] * (
        (jnp.roll(interior, -1, 2) - jnp.roll(interior, 1, 2)) * 0.5
    )
    along_div = (jnp.roll(along_flux, -1, 2) - jnp.roll(along_flux, 1, 2)) * 0.5
    return (interior, depth_div + across_div + along_div)


def shards(wave_coeff, response_coeff, band_index, occupation, local_kernel, gradient_kernel):
    length = wave_coeff.shape[2]
    band_count = wave_coeff.shape[0]
    slab_count = lax.axis_size("slab")
    pool_count = lax.axis_size("pool")
    planes = length // slab_count
    columns = length // pool_count
    slab_width = length // slab_count
    slab_rank = lax.axis_index("slab")
    pool_rank = lax.axis_index("pool")
    first_row = pool_rank * columns
    factor = 1.0 / occupation.shape[0]
    inverse_half = stacked_table(length, 1.0, jnp.bfloat16)
    forward_full = stacked_table(length, -1.0, jnp.float32)
    inverse_full = stacked_table(length, 1.0, jnp.float32)
    weights = band_weights(band_index, occupation)
    cube_shape = (band_count, 2, length, length, length)
    wave_planes = half_pass(
        "rzsk,bskxy->brzxy", inverse_half, wave_coeff.reshape(cube_shape)
    ).astype(jnp.bfloat16)
    response_planes = half_pass(
        "rzsk,bskxy->brzxy", inverse_half, response_coeff.reshape(cube_shape)
    ).astype(jnp.bfloat16)
    wave_rows = half_pass("rxsk,bszky->brzxy", inverse_half, wave_planes).astype(jnp.bfloat16)
    response_rows = half_pass("rxsk,bszky->brzxy", inverse_half, response_planes).astype(
        jnp.bfloat16
    )
    wave_space = half_pass("rysk,bszxk->brxzy", inverse_half, wave_rows)
    response_space = half_pass("rysk,bszxk->brxzy", inverse_half, response_rows)
    pool_part = lax.psum_scatter(
        weighted_intersection(wave_space, response_space, weights, factor).reshape(
            columns * lax.axis_size("pool"), length * length
        ),
        "pool",
        scatter_dimension=0,
        tiled=True,
    )
    shared = lax.psum_scatter(
        pool_part.reshape(columns, length, length), "slab", scatter_dimension=1, tiled=True
    )
    density_block = jnp.transpose(shared, (1, 0, 2))
    slab_density = lax.all_gather(density_block, "pool", axis=1, tiled=True)
    complex_slab = jnp.stack([slab_density, jnp.zeros_like(slab_density)])
    spectrum = exact_pass(
        "rxsk,szky->rzxy", forward_full, exact_pass("rysk,szxk->rzxy", forward_full, complex_slab)
    )
    turned = lax.all_to_all(spectrum, "slab", split_axis=2, concat_axis=1, tiled=True)
    kernel = coulomb_kernel(length, (0, slab_rank * slab_width, 0), (length, slab_width, length))
    scaled = exact_pass("rzsk,skxy->rzxy", forward_full, turned) * kernel[None]
    returned = lax.all_to_all(
        exact_pass("rzsk,skxy->rzxy", inverse_full, scaled),
        "slab",
        split_axis=1,
        concat_axis=2,
        tiled=True,
    )
    potential_slab = exact_pass(
        "rysk,szxk->rzxy", inverse_full[0:1], exact_pass("rxsk,szky->rzxy", inverse_full, returned)
    )[0]
    hartree = lax.dynamic_slice_in_dim(potential_slab, first_row, columns, 1)
    gradient_slab = gradient_kernel.reshape(planes, length, length)
    padded_density, padded_coefficient = (
        extended_2(slab_density, (("slab", 0),), 2),
        extended_2(gradient_slab, (("slab", 0),), 2),
    )
    padded_density = wrapped_window(padded_density, first_row, columns)
    padded_coefficient = wrapped_window(padded_coefficient, first_row, columns)
    local_block = lax.dynamic_slice_in_dim(
        local_kernel.reshape(planes, length, length), first_row, columns, 1
    )
    interior, divergence = flux_divergence(padded_density, padded_coefficient)
    potential = hartree + local_block * interior - divergence
    return potential.reshape(planes, columns * length)


def solution(mesh):
    return jax.shard_map(
        shards,
        mesh=mesh,
        in_specs=(
            P(("pool", "slab"), None, None, None),
            P(("pool", "slab"), None, None, None),
            P(("pool", "slab")),
            P(),
            P("slab", None),
            P("slab", None),
        ),
        out_specs=P("slab", "pool"),
        check_vma=False,
    )
```

profile of v0, /device:TPU:0, one launch (start us, length us, event | category | flops | bytes accessed | tf_op | source)
XLA Modules:
  0.0 262.5 jit_solution(9596390808301206953)
XLA Ops:
  7.2 7.8 %reshape.229 = bf16[2,96,96,96]{3,2,1,0:T(8,128)(2,1)} reshape(bf16[1,2,96,9216]{3,2,1,0:T(8,128)(2,1)} %param.7) | data formatting | bytes 7077888 | tf_op jit(solution)/shard_map/reshape.15
  15.1 6.9 %fusion.4 = bf16[2,96,96,96,1]{3,1,2,0,4:T(8,128)(2,1)} fusion(bf16[2,96,96,96]{3,2,1,0:T(8,128)(2,1)} %reshape.229, bf16[2,96,2,96]{3,1,2,0:T(8,128)(2,1)S(1)} %fusion.62), kind=kOutput, calls=%fused_computation.7 | convolution fusion | flops 681246720 | bytes 7151616 | tf_op jit(solution)/shard_map/rzsk,bskxy->brzxy/dot_general | solution.py:59
  22.0 8.9 %fusion.21 = f32[1,2,96,96,96]{4,2,1,3,0:T(8,128)} fusion(bf16[2,96,96,96,1]{3,1,2,0,4:T(8,128)(2,1)} %fusion.4, bf16[2,96,2,96]{3,1,2,0:T(8,128)(2,1)S(1)} %fusion.62), kind=kOutput, calls=%fused_computation.25 | convolution fusion | flops 1360723968 | bytes 10690560 | tf_op jit(solution)/shard_map/rysk,bszxk->brxzy/dot_general | solution.py:59
  30.9 7.8 %reshape.227 = bf16[2,96,96,96]{3,2,1,0:T(8,128)(2,1)} reshape(bf16[1,2,96,9216]{3,2,1,0:T(8,128)(2,1)} %param.6) | data formatting | bytes 7077888 | tf_op jit(solution)/shard_map/reshape.2
  38.7 6.9 %fusion = bf16[2,96,96,96,1]{3,1,2,0,4:T(8,128)(2,1)} fusion(bf16[2,96,96,96]{3,2,1,0:T(8,128)(2,1)} %reshape.227, bf16[2,96,2,96]{3,1,2,0:T(8,128)(2,1)S(1)} %fusion.62), kind=kOutput, calls=%fused_computation.4 | convolution fusion | flops 681246720 | bytes 7151616 | tf_op jit(solution)/shard_map/rzsk,bskxy->brzxy/dot_general | solution.py:59
  45.6 8.8 %fusion.24 = f32[1,2,96,96,96]{4,2,1,3,0:T(8,128)} fusion(bf16[2,96,96,96,1]{3,1,2,0,4:T(8,128)(2,1)} %fusion, bf16[2,96,2,96]{3,1,2,0:T(8,128)(2,1)S(1)} %fusion.62), kind=kOutput, calls=%fused_computation.26 | convolution fusion | flops 1360723968 | bytes 10690560 | tf_op jit(solution)/shard_map/rysk,bszxk->brxzy/dot_general | solution.py:59
  56.2 7.8 %fusion.10 = f32[1,1,96,96,96]{4,2,1,3,0:T(8,128)S(1)} fusion(f32[1,2,96,96,96]{4,2,1,3,0:T(8,128)} %fusion.21, f32[1,2,96,96,96]{4,2,1,3,0:T(8,128)} %fusion.24, f32[]{:T(128)S(6)} %convert_element_type.93), kind=kLoop, calls=%fused_computation.13 | loop fusion | flops 4423680 | bytes 17694724 | tf_op jit(solution)/shard_map/mul | solution.py:70
  64.0 4.9 %copy.41 = f32[1,1,96,96,96]{4,3,2,1,0:T(8,128)} copy(f32[1,1,96,96,96]{4,2,1,3,0:T(8,128)S(1)} %fusion.10) | data formatting | bytes 7077888 | tf_op jit(solution)/shard_map/mul | solution.py:70
  68.9 6.1 %mul.320 = f32[96,9216]{1,0:T(8,128)} reshape(f32[1,1,96,96,96]{4,3,2,1,0:T(8,128)} %copy.41) | data formatting | bytes 7077888 | tf_op jit(solution)/shard_map/mul | solution.py:70
  75.1 50.0 %reduce-scatter.7.cloned.1.call-done = f32[24,9216]{1,0:T(8,128)} async-done(((f32[96,9216]{1,0:T(8,128)}), f32[24,9216]{1,0:T(8,128)}) %reduce-scatter.7.cloned.1.call-update) | async-done | bytes 884752
  131.1 3.5 %collective-permute-start.3 = (f32[2,96,96]{2,1,0:T(8,128)}, f32[2,96,96]{2,1,0:T(8,128)S(1)}, u32[]{:S(2)}, u32[]{:S(2)}) collective-permute-start(f32[2,96,96]{2,1,0:T(8,128)} %slice.122), channel_id=1, source_target_pairs={{1,0},{2,1},{3,2},{4,3},{5,4},{6,5},{7,6},{0,7},{9,8},{10,9},{11,1... | collective-permute-start | bytes 221192 | tf_op jit(solution)/shard_map/ppermute | solution.py:19
  134.7 27.6 %reduce-scatter.5.cloned.1.call-done = f32[24,12,96]{2,0,1:T(8,128)} async-done(((f32[24,96,96]{2,0,1:T(8,128)}), f32[24,12,96]{2,0,1:T(8,128)}) %reduce-scatter.5.cloned.1.call-update) | async-done | bytes 110608 | tf_op jit(solution)/shard_map/reduce_scatter | solution.py:128
  162.4 11.1 %all_gather.3 = f32[12,96,96]{2,1,0:T(8,128)S(1)} all-gather(f32[12,24,96]{2,1,0:T(8,128)} %bitcast.184), channel_id=1, replica_groups=mesh['pool'=4,'slab'=8] {'pool'}, dimensions={1}, use_global_device_ids=true | all-gather | bytes 552960 | tf_op jit(solution)/shard_map/all_gather | solution.py:132
  174.6 2.0 convolution_bitcast_fusion.3
  178.0 3.6 %all-to-all-start = ((f32[2,12,96,96]{3,0,1,2:T(2,128)}), f32[2,12,96,96]{3,0,1,2:T(2,128)S(1)}, u32[]{:S(2)}, u32[]{:S(2)}) async-start(f32[2,12,96,96]{3,0,1,2:T(2,128)} %copy.44), calls=%async_computation.1 | async-start | bytes 2359296 | tf_op jit(solution)/shard_map/all_to_all | solution.py:137
  183.1 2.1 reshape.232
  186.7 3.4 %collective-permute-start.1 = (f32[2,96,96]{2,1,0:T(8,128)S(1)}, f32[2,96,96]{2,1,0:T(8,128)S(1)}, u32[]{:S(2)}, u32[]{:S(2)}) collective-permute-start(f32[2,96,96]{2,1,0:T(8,128)S(1)} %get-tuple-element.11), channel_id=1, source_target_pairs={{1,0},{2,1},{3,2},{4,3},{5,4},{6,5},{7,6},{0,7},{9,8},{10,9},{11,1... | collective-permute-start | bytes 221192 | tf_op jit(solution)/shard_map/ppermute | solution.py:19
  190.2 17.0 %collective-permute-done = f32[2,96,96]{2,1,0:T(8,128)S(1)} collective-permute-done((f32[2,96,96]{2,1,0:T(8,128)S(1)}, f32[2,96,96]{2,1,0:T(8,128)S(1)}, u32[]{:S(2)}, u32[]{:S(2)}) %collective-permute-start) | collective-permute-done | bytes 73760 | tf_op jit(solution)/shard_map/ppermute | solution.py:18
  207.5 4.5 %all-to-all-done = f32[2,12,96,96]{3,0,1,2:T(2,128)S(1)} async-done(((f32[2,12,96,96]{3,0,1,2:T(2,128)}), f32[2,12,96,96]{3,0,1,2:T(2,128)S(1)}, u32[]{:S(2)}, u32[]{:S(2)}) %all-to-all-start) | async-done | bytes 884768 | tf_op jit(solution)/shard_map/all_to_all | solution.py:137
  214.8 1.9 copy.48
  216.7 3.6 %all-to-all-start.1 = ((f32[2,96,12,96]{3,0,2,1:T(2,128)}), f32[2,96,12,96]{3,0,2,1:T(2,128)S(1)}, u32[]{:S(2)}, u32[]{:S(2)}) async-start(f32[2,96,12,96]{3,0,2,1:T(2,128)} %copy.48), calls=%async_computation.2 | async-start | bytes 2359296 | tf_op jit(solution)/shard_map/all_to_all | solution.py:140
  221.0 28.6 %all-to-all-done.1 = f32[2,96,12,96]{3,0,2,1:T(2,128)S(1)} async-done(((f32[2,96,12,96]{3,0,2,1:T(2,128)}), f32[2,96,12,96]{3,0,2,1:T(2,128)S(1)}, u32[]{:S(2)}, u32[]{:S(2)}) %all-to-all-start.1) | async-done | bytes 884768 | tf_op jit(solution)/shard_map/all_to_all | solution.py:140
  249.7 2.1 convolution_bitcast_fusion
  251.8 2.0 convolution_bitcast_fusion.5
  (52 shorter events, 18.7 us)
Async XLA Ops:
  6.5 118.5 %reduce-scatter.7.cloned.1.call-start = ((), (), s32[]{:S(2)}) async-start(), calls=%async_computation.5 | async-start | bytes 4423680
  45.6 9.5 %copy-start = (s32[32]{0:T(128)S(1)}, s32[32]{0:T(128)}, u32[]{:S(2)}) copy-start(s32[32]{0:T(128)} %param.9) | copy-start | bytes 388
  75.0 87.4 %reduce-scatter.5.cloned.1.call-start = ((), (), s32[]{:S(2)}) async-start(), calls=%async_computation.4 | async-start | bytes 1327104 | tf_op jit(solution)/shard_map/reduce_scatter | solution.py:128
  130.3 54.9 %collective-permute-start.2 = (f32[2,96,96]{2,1,0:T(8,128)}, f32[2,96,96]{2,1,0:T(8,128)}, u32[]{:S(2)}, u32[]{:S(2)}) collective-permute-start(f32[2,96,96]{2,1,0:T(8,128)} %slice.120), channel_id=1, source_target_pairs={{0,1},{1,2},{2,3},{3,4},{4,5},{5,6},{6,7},{7,0},{8,9},{9,10},{10,1... | collective-permute-start | bytes 221192 | tf_op jit(solution)/shard_map/ppermute | solution.py:18
  131.1 55.1 %collective-permute-start.3 = (f32[2,96,96]{2,1,0:T(8,128)}, f32[2,96,96]{2,1,0:T(8,128)S(1)}, u32[]{:S(2)}, u32[]{:S(2)}) collective-permute-start(f32[2,96,96]{2,1,0:T(8,128)} %slice.122), channel_id=1, source_target_pairs={{1,0},{2,1},{3,2},{4,3},{5,4},{6,5},{7,6},{0,7},{9,8},{10,9},{11,1... | collective-permute-start | bytes 221192 | tf_op jit(solution)/shard_map/ppermute | solution.py:19
  178.0 33.9 %all-to-all-start = ((f32[2,12,96,96]{3,0,1,2:T(2,128)}), f32[2,12,96,96]{3,0,1,2:T(2,128)S(1)}, u32[]{:S(2)}, u32[]{:S(2)}) async-start(f32[2,12,96,96]{3,0,1,2:T(2,128)} %copy.44), calls=%async_computation.1 | async-start | bytes 2359296 | tf_op jit(solution)/shard_map/all_to_all | solution.py:137
  186.3 20.8 %collective-permute-start = (f32[2,96,96]{2,1,0:T(8,128)S(1)}, f32[2,96,96]{2,1,0:T(8,128)S(1)}, u32[]{:S(2)}, u32[]{:S(2)}) collective-permute-start(f32[2,96,96]{2,1,0:T(8,128)S(1)} %get-tuple-element.12), channel_id=1, source_target_pairs={{0,1},{1,2},{2,3},{3,4},{4,5},{5,6},{6,7},{7,0},{8,9},{9,10},{10,1... | collective-permute-start | bytes 221192 | tf_op jit(solution)/shard_map/ppermute | solution.py:18
  186.7 20.4 %collective-permute-start.1 = (f32[2,96,96]{2,1,0:T(8,128)S(1)}, f32[2,96,96]{2,1,0:T(8,128)S(1)}, u32[]{:S(2)}, u32[]{:S(2)}) collective-permute-start(f32[2,96,96]{2,1,0:T(8,128)S(1)} %get-tuple-element.11), channel_id=1, source_target_pairs={{1,0},{2,1},{3,2},{4,3},{5,4},{6,5},{7,6},{0,7},{9,8},{10,9},{11,1... | collective-permute-start | bytes 221192 | tf_op jit(solution)/shard_map/ppermute | solution.py:19
  216.7 32.9 %all-to-all-start.1 = ((f32[2,96,12,96]{3,0,2,1:T(2,128)}), f32[2,96,12,96]{3,0,2,1:T(2,128)S(1)}, u32[]{:S(2)}, u32[]{:S(2)}) async-start(f32[2,96,12,96]{3,0,2,1:T(2,128)} %copy.48), calls=%async_computation.2 | async-start | bytes 2359296 | tf_op jit(solution)/shard_map/all_to_all | solution.py:140
Sparse Core Ops, SparseCore 0:
  75.1 49.8 reduce-scatter.6
  128.6 33.7 reduce-scatter.4
where the time goes:
time: 263 us
  waiting for transfers between devices  128 us (49%)
  local copies, waits for them, and re-layouts  42.1 us (16%)
  matrix products  41.2 us (16%)
  between operations  14.9 us (6%)
  starting transfers between devices  14.6 us (6%)
  blocking collectives  11.1 us (4%)
  other arithmetic  10.9 us (4%)
    unnamed x3, waiting for transfers between devices  50 us
    dot_general x4, matrix products, half_pass(): return jnp.einsum(spec, tables, values, preferred_element_type=jnp.float32)  31.5 us
    all_to_all x1, waiting for transfers between devices, shards(): lax.all_to_all(exact_pass('rzsk,skxy->rzxy', inverse_full, scaled), 'slab...  28.6 us
    reduce_scatter x1, waiting for transfers between devices, shards(): lax.psum_scatter(pool_part.reshape(columns, length, length), 'slab', scat...  27.6 us
    ppermute x2, waiting for transfers between devices, extended_2(): before = lax.ppermute(last, axis, up)  17 us
    another operation x2, local copies, waits for them, and re-layouts  15.7 us
    all_gather x1, blocking collectives, shards(): slab_density = lax.all_gather(density_block, 'pool', axis=1, tiled=True)  11.1 us
    mul x2, local copies, waits for them, and re-layouts, weighted_intersection(): return jnp.sum(weights[:, None, None, None] * intersection, axis=0) * factor  11 us
  transfers between devices with their start and end apart: 8, of which 5 were waited for; matrix products, arithmetic and copies ran while one was open for 5% of the time, Pallas kernels for 0%

commit v1 on v0

v1 whole, which is shorter than its diff:
```python
import functools
import math

import jax
import jax.numpy as jnp
import numpy as np
from jax import lax
from jax.experimental import pallas as pl
from jax.experimental.pallas import tpu as pltpu
from jax.sharding import PartitionSpec as P

full_turn = 2.0 * math.pi
MESH = pl.DeviceIdType.MESH


def stacked_table(length, sign, dtype):
    indices = jnp.arange(length, dtype=jnp.int32)
    product = indices[:, None] * indices[None, :] % length
    angles = product.astype(jnp.float32) * (full_turn / length)
    factor = 1.0 / math.sqrt(length)
    cosine = jnp.cos(angles) * factor
    sine_part = jnp.sin(angles) * factor
    upper_half = jnp.stack([cosine, -sign * sine_part], axis=1)
    lower_half = jnp.stack([sign * sine_part, cosine], axis=1)
    return jnp.stack([upper_half, lower_half], axis=0).astype(dtype)


def signed_freq(length, first_wave, amount):
    waves = first_wave + jnp.arange(amount, dtype=jnp.int32)
    return jnp.where(2 * waves >= length, waves - length, waves).astype(jnp.float32)


def exact_pass(spec, tables, values):
    return jnp.einsum(
        spec, tables, values, precision=lax.Precision.HIGHEST, preferred_element_type=jnp.float32
    )


def half_pass(spec, tables, values):
    return jnp.einsum(spec, tables, values, preferred_element_type=jnp.float32)


def band_weights(band_index, occupation):
    numbers = jnp.arange(occupation.shape[0], dtype=jnp.int32)
    matches = band_index[:, None] == numbers[None, :]
    return jnp.sum(jnp.where(matches, occupation[None, :], 0), axis=1).astype(jnp.float32)


def weighted_intersection(wave_space, response_space, weights, factor):
    intersection = wave_space[:, 0] * response_space[:, 0] + wave_space[:, 1] * response_space[:, 1]
    return jnp.sum(weights[:, None, None, None] * intersection, axis=0) * factor


def wrapped_window(block, first_row, width):
    extended = jnp.concatenate([block[:, -2:], block, block[:, :2]], axis=1)
    return lax.dynamic_slice_in_dim(extended, first_row, width + 4, 1)


def band_density(wave_coeff, response_coeff, weights, factor, slab_count, pool_count):
    length = wave_coeff.shape[2]
    cube_shape = (wave_coeff.shape[0], 2, length, length, length)
    inverse_half = stacked_table(length, 1.0, jnp.bfloat16)

    def to_space(coeff):
        planes = half_pass("rzsk,bskxy->brzxy", inverse_half, coeff.reshape(cube_shape)).astype(
            jnp.bfloat16
        )
        rows = half_pass("rxsk,bszky->brzxy", inverse_half, planes).astype(jnp.bfloat16)
        return half_pass("rysk,bszxk->brzxy", inverse_half, rows)

    density = weighted_intersection(to_space(wave_coeff), to_space(response_coeff), weights, factor)
    density = density.reshape(
        slab_count, length // slab_count, pool_count, length // pool_count, length
    )
    return jnp.transpose(density, (0, 2, 1, 3, 4)).reshape(slab_count, pool_count, -1, length)


def block_order(slab_rank, chips):
    return [lax.rem(slab_rank // 2 + step, chips) for step in list(range(1, chips)) + [0]]


def greet(devices):
    barrier = pltpu.get_barrier_semaphore()
    for device in devices:
        pl.semaphore_signal(barrier, inc=1, device_id=device, device_id_type=MESH)
    pl.semaphore_wait(barrier, len(devices))


def reduce_kernel(pools, slabs, part, full, first, second, own, third, gathered, sems_a, sems_b, sems_c, sems_d):
    pool = lax.axis_index("pool")
    slab = lax.axis_index("slab")
    chips = slabs // 2
    core = lax.rem(slab, 2)
    chip = slab // 2
    twin = (pool, 2 * chip + 1 - core)
    mates = [(lax.rem(pool + d, pools), slab) for d in range(1, pools)]
    column = [(pool, 2 * lax.rem(chip + e, chips) + core) for e in range(1, chips)]
    greet([twin] + mates + column)
    order = block_order(slab, chips)
    swaps = []
    for i, t in enumerate(order):
        copy = pltpu.make_async_remote_copy(
            src_ref=part.at[2 * t + 1 - core],
            dst_ref=first.at[i],
            send_sem=sems_a.at[0, i],
            recv_sem=sems_a.at[1, i],
            device_id=twin,
            device_id_type=MESH,
        )
        copy.start()
        swaps.append(copy)
    spreads = []
    for i, t in enumerate(order):
        swaps[i].wait()
        for q in range(pools):
            first[i, q] = first[i, q] + part[2 * t + core, q]
        row = []
        for d in range(1, pools):
            copy = pltpu.make_async_remote_copy(
                src_ref=first.at[i, lax.rem(pool + d, pools)],
                dst_ref=second.at[i, d - 1],
                send_sem=sems_b.at[0, i, d - 1],
                recv_sem=sems_b.at[1, i, d - 1],
                device_id=mates[d - 1],
                device_id_type=MESH,
            )
            copy.start()
            row.append(copy)
        spreads.append(row)
    lifts = []
    for i in range(chips):
        total = first[i, pool]
        for d, copy in enumerate(spreads[i]):
            copy.wait()
            total = total + second[i, d]
        own[i] = total
        if i < chips - 1:
            copy = pltpu.make_async_remote_copy(
                src_ref=own.at[i],
                dst_ref=third.at[i],
                send_sem=sems_c.at[0, i],
                recv_sem=sems_c.at[1, i],
                device_id=column[i],
                device_id_type=MESH,
            )
            copy.start()
            lifts.append(copy)
    total = own[chips - 1]
    for i, copy in enumerate(lifts):
        copy.wait()
        total = total + third[i]
    gathered[0] = total
    sends = []
    for d in range(1, pools):
        copy = pltpu.make_async_remote_copy(
            src_ref=gathered.at[0],
            dst_ref=gathered.at[d],
            send_sem=sems_d.at[0, d - 1],
            recv_sem=sems_d.at[1, d - 1],
            device_id=mates[d - 1],
            device_id_type=MESH,
        )
        copy.start()
        sends.append(copy)
    full[pool] = total
    for d in range(1, pools):
        sends[d - 1].wait()
        full[lax.rem(pool + pools - d, pools)] = gathered[d]


def reduce_density(part):
    slabs, pools, rows, lanes = part.shape
    chips = slabs // 2
    vmem = pl.BlockSpec(memory_space=pltpu.VMEM)
    return pl.pallas_call(
        functools.partial(reduce_kernel, pools, slabs),
        out_shape=jax.ShapeDtypeStruct((pools, rows, lanes), jnp.float32),
        in_specs=[vmem],
        out_specs=vmem,
        scratch_shapes=[
            pltpu.VMEM((chips, pools, rows, lanes), jnp.float32),
            pltpu.VMEM((chips, pools - 1, rows, lanes), jnp.float32),
            pltpu.VMEM((chips, rows, lanes), jnp.float32),
            pltpu.VMEM((chips - 1, rows, lanes), jnp.float32),
            pltpu.VMEM((pools, rows, lanes), jnp.float32),
            pltpu.SemaphoreType.DMA((2, chips)),
            pltpu.SemaphoreType.DMA((2, chips, pools - 1)),
            pltpu.SemaphoreType.DMA((2, chips - 1)),
            pltpu.SemaphoreType.DMA((2, pools - 1)),
        ],
        compiler_params=pltpu.CompilerParams(
            collective_id=0, has_side_effects=True, vmem_limit_bytes=56 * 2**20
        ),
    )(part)


def high_dot(a, b):
    return lax.dot_general(
        a,
        b,
        (((1,), (0,)), ((), ())),
        precision=lax.Precision.HIGHEST,
        preferred_element_type=jnp.float32,
    )


def screen_kernel(
    pools, slabs, spec, ahead, back, coulomb, edges, full, halos,
    landed, turned, returned, gathered, sems_a, sems_b, sems_c, sems_d,
):
    pool = lax.axis_index("pool")
    slab = lax.axis_index("slab")
    mates = [(lax.rem(pool + d, pools), slab) for d in range(1, pools)]
    column = [(pool, lax.rem(slab + e, slabs)) for e in range(1, slabs)]
    greet(mates + column)
    hops = slabs - 1

    def send(src, dst, sems, i, device):
        copy = pltpu.make_async_remote_copy(
            src_ref=src,
            dst_ref=dst,
            send_sem=sems.at[0, i],
            recv_sem=sems.at[1, i],
            device_id=device,
            device_id_type=MESH,
        )
        copy.start()
        return copy

    copies = [
        send(spec.at[lax.rem(slab + e, slabs)], landed.at[slab], sems_a, e - 1, column[e - 1])
        for e in range(1, slabs)
    ]
    rims = [
        send(edges.at[0], halos.at[0], sems_d, 0, column[0]),
        send(edges.at[1], halos.at[1], sems_d, 1, column[hops - 1]),
    ]
    landed[slab] = spec[slab]
    for copy in copies:
        copy.wait()
    kxs, zp, lanes = spec.shape[1:]
    length = coulomb.shape[1]
    sign = jnp.where(lax.broadcasted_iota(jnp.int32, (1, lanes), 1) < lanes // 2, 1.0, -1.0)
    for j in range(kxs):
        values = landed[:, j].reshape(slabs * zp, lanes)
        out = high_dot(ahead[...], values)
        mixed = out[:length] + sign * pltpu.roll(out[length:], lanes // 2, 1)
        mixed = mixed * coulomb[j]
        out = high_dot(back[...], mixed)
        half = slabs * zp
        mixed = out[:half] - sign * pltpu.roll(out[half:], lanes // 2, 1)
        turned[:, j] = mixed.reshape(slabs, zp, lanes)
    copies = [
        send(turned.at[lax.rem(slab + e, slabs)], returned.at[slab], sems_b, e - 1, column[e - 1])
        for e in range(1, slabs)
    ]
    returned[slab] = turned[slab]
    for copy in copies:
        copy.wait()
    copies = [
        send(returned, gathered.at[d - 1], sems_c, d - 1, mates[d - 1]) for d in range(1, pools)
    ]
    full[pool] = returned[...]
    for d in range(1, pools):
        copies[d - 1].wait()
        full[lax.rem(pool + pools - d, pools)] = gathered[d - 1]
    for copy in rims:
        copy.wait()


def screened(spec, ahead, back, coulomb, edges, pools):
    slabs, kxs, zp, lanes = spec.shape
    vmem = pl.BlockSpec(memory_space=pltpu.VMEM)
    return pl.pallas_call(
        functools.partial(screen_kernel, pools, slabs),
        out_shape=(
            jax.ShapeDtypeStruct((pools, slabs, kxs, zp, lanes), jnp.float32),
            jax.ShapeDtypeStruct(edges.shape, jnp.float32),
        ),
        in_specs=[vmem] * 5,
        out_specs=(vmem, vmem),
        scratch_shapes=[
            pltpu.VMEM((slabs, kxs, zp, lanes), jnp.float32),
            pltpu.VMEM((slabs, kxs, zp, lanes), jnp.float32),
            pltpu.VMEM((slabs, kxs, zp, lanes), jnp.float32),
            pltpu.VMEM((pools - 1, slabs, kxs, zp, lanes), jnp.float32),
            pltpu.SemaphoreType.DMA((2, slabs - 1)),
            pltpu.SemaphoreType.DMA((2, slabs - 1)),
            pltpu.SemaphoreType.DMA((2, pools - 1)),
            pltpu.SemaphoreType.DMA((2, 2)),
        ],
        compiler_params=pltpu.CompilerParams(
            collective_id=1, has_side_effects=True, vmem_limit_bytes=40 * 2**20
        ),
    )(spec, ahead, back, coulomb, edges)


def waves(length):
    index = np.arange(length)
    angle = (index[:, None] * index[None, :] % length) * (full_turn / length)
    return np.cos(angle) / math.sqrt(length), np.sin(angle) / math.sqrt(length)


def hartree_tables(length, pools, slabs):
    cosine, sine = waves(length)
    planes, kxn = length // slabs, length // pools
    zp = -(-planes // 8) * 8
    kxs = -(-kxn // slabs)
    padded = kxs * slabs
    half = length // 2 + 1
    lanes = 128
    mid = lanes // 2
    y_ahead = np.zeros((length, lanes))
    y_ahead[:, :half] = cosine[:, :half]
    y_ahead[:, mid : mid + half] = -sine[:, :half]
    weight = np.full((half, 1), 2.0)
    weight[0] = 1.0
    if length % 2 == 0:
        weight[-1] = 1.0
    y_back = np.zeros((lanes, length))
    y_back[:half] = weight * cosine[:half]
    y_back[mid : mid + half] = -weight * sine[:half]
    x_ahead = np.zeros((pools, 2, padded, length))
    x_back = np.zeros((pools, 2, kxn, pools, padded))
    for r, table in enumerate((cosine, sine)):
        x_ahead[:, r, :kxn] = table.reshape(pools, kxn, length)
        x_back[:, r, :, :, :kxn] = table.reshape(pools, kxn, pools, kxn)
    z_ahead = np.zeros((2, length, slabs, zp))
    z_back = np.zeros((2, slabs, zp, length))
    for r, table in enumerate((cosine, sine)):
        z_ahead[r, :, :, :planes] = table.reshape(length, slabs, planes)
        z_back[r, :, :planes] = table.reshape(slabs, planes, length)
    z_ahead = z_ahead.reshape(2 * length, slabs * zp)
    z_back = z_back.reshape(2 * slabs * zp, length)
    tables = (y_ahead, y_back, x_ahead, x_back, z_ahead, z_back)
    return [jnp.asarray(t.astype(np.float32)) for t in tables]


def shards(wave_coeff, response_coeff, band_index, occupation, local_kernel, gradient_kernel):
    length = wave_coeff.shape[2]
    band_count = wave_coeff.shape[0]
    slab_count = lax.axis_size("slab")
    pool_count = lax.axis_size("pool")
    planes = length // slab_count
    columns = length // pool_count
    slab_rank = lax.axis_index("slab")
    pool_rank = lax.axis_index("pool")
    first_row = pool_rank * columns
    factor = 1.0 / occupation.shape[0]
    y_ahead, y_back, x_ahead, x_back, z_ahead, z_back = hartree_tables(
        length, pool_count, slab_count
    )
    weights = band_weights(band_index, occupation)
    part = band_density(wave_coeff, response_coeff, weights, factor, slab_count, pool_count)
    blocks = reduce_density(part).reshape(pool_count, planes, columns, length)

    lanes = y_ahead.shape[1]
    sign = jnp.where(jnp.arange(lanes) < lanes // 2, 1.0, -1.0).astype(jnp.float32)
    along = exact_pass("qzxy,yl->qzxl", blocks, y_ahead)
    turn = x_ahead[pool_rank].reshape(2, -1, pool_count, columns)
    both = exact_pass("rkqx,qzxl->rkzl", turn, along)
    spec = both[0] + sign * jnp.roll(both[1], lanes // 2, 2)
    zp = z_ahead.shape[1] // slab_count
    kxs = spec.shape[0] // slab_count
    spec = jnp.pad(spec, ((0, 0), (0, zp - planes), (0, 0)))
    spec = spec.reshape(slab_count, kxs, zp, lanes)
    kx = signed_freq(length, pool_rank * columns + slab_rank * kxs, kxs)[:, None, None]
    kz = signed_freq(length, 0, length)[None, :, None]
    ky = (jnp.arange(lanes) % (lanes // 2)).astype(jnp.float32)[None, None, :]
    squared = (full_turn / length) ** 2 * (kz * kz + kx * kx + ky * ky)
    coulomb = jnp.where(squared > 0, full_turn / jnp.where(squared > 0, squared, 1.0), 0.0)

    interior = blocks[pool_rank]
    gradient = gradient_kernel.reshape(planes, length, length)
    gradient_own = lax.dynamic_slice_in_dim(gradient, first_row, columns, 1)
    edges = jnp.stack(
        [
            jnp.concatenate([interior[-2:], gradient_own[-1:]]),
            jnp.concatenate([interior[:2], gradient_own[:1]]),
        ]
    )
    returned, halos = screened(spec, z_ahead, z_back, coulomb, edges, pool_count)

    tall = jnp.concatenate([halos[0, :2], interior, halos[1, :2]], axis=0)
    tall_gradient = jnp.concatenate([halos[0, 2:], gradient_own, halos[1, 2:]], axis=0)
    depth_flux = tall_gradient * ((tall[2:] - tall[:-2]) * 0.5)
    depth_div = (depth_flux[2:] - depth_flux[:-2]) * 0.5
    slab_density = jnp.transpose(blocks, (1, 0, 2, 3)).reshape(planes, length, length)
    wide = wrapped_window(slab_density, first_row, columns)
    wide_gradient = wrapped_window(gradient, first_row, columns)[:, 1:-1]
    across_flux = wide_gradient * ((wide[:, 2:] - wide[:, :-2]) * 0.5)
    across_div = (across_flux[:, 2:] - across_flux[:, :-2]) * 0.5
    along_flux = gradient_own * ((jnp.roll(interior, -1, 2) - jnp.roll(interior, 1, 2)) * 0.5)
    along_div = (jnp.roll(along_flux, -1, 2) - jnp.roll(along_flux, 1, 2)) * 0.5
    local_block = lax.dynamic_slice_in_dim(
        local_kernel.reshape(planes, length, length), first_row, columns, 1
    )
    rest = local_block * interior - (depth_div + across_div + along_div)

    returned = returned.reshape(pool_count, kxs * slab_count, zp, lanes)[:, :, :planes]
    both = exact_pass("rxpk,pkzl->rzxl", x_back[pool_rank], returned)
    across = both[0] - sign * jnp.roll(both[1], lanes // 2, 2)
    potential = exact_pass("zxl,ly->zxy", across, y_back) + rest
    return potential.reshape(planes, columns * length)


def solution(mesh):
    return jax.shard_map(
        shards,
        mesh=mesh,
        in_specs=(
            P(("pool", "slab"), None, None, None),
            P(("pool", "slab"), None, None, None),
            P(("pool", "slab")),
            P(),
            P("slab", None),
            P("slab", None),
        ),
        out_specs=P("slab", "pool"),
        check_vma=False,
    )
```

time: 263 us -> 153 us (0.58)
  waiting for transfers between devices: 128 us -> 0 us
  Pallas kernels: 0 us -> 72.9 us
  starting transfers between devices: 14.6 us -> 0 us
  between operations: 14.9 us -> 1.71 us
  blocking collectives: 11.1 us -> 0 us
  matrix products: 41.2 us -> 31.7 us
  local copies, waits for them, and re-layouts: 42.1 us -> 36.3 us
    pallas_call x0 -> x2, Pallas kernels: none -> 72.9 us  [the longest x1 47.1 us: reduce_density(): pl.pallas_call(functools.partial(reduce_kernel, pools, slabs), out_shape=...]
    unnamed x3 -> x0, waiting for transfers between devices: 50 us -> none
    all_to_all x2 -> x0, waiting for transfers between devices: 33.1 us -> none  [the longest x1 28.6 us: shards(): lax.all_to_all(exact_pass('rzsk,skxy->rzxy', inverse_full, scaled), 'slab...]
    reduce_scatter x1 -> x0, waiting for transfers between devices: 27.6 us -> none  [shards(): lax.psum_scatter(pool_part.reshape(columns, length, length), 'slab', scat...]
    ppermute x4 -> x0, waiting for transfers between devices: 17 us -> none  [the longest x2 17 us: extended_2(): before = lax.ppermute(last, axis, up)]
    dot_general x1 -> x2, local copies, waits for them, and re-layouts: 1.94 us -> 15 us  [half_pass(): return jnp.einsum(spec, tables, values, preferred_element_type=jnp.float32)]
    all_gather x1 -> x0, blocking collectives: 11.1 us -> none  [shards(): slab_density = lax.all_gather(density_block, 'pool', axis=1, tiled=True)]
    mul x2 -> x1, local copies, waits for them, and re-layouts: 11 us -> 2.72 us  [weighted_intersection(): return jnp.sum(weights[:, None, None, None] * intersection, axis=0) * factor]
  transfers between devices with their start and end apart: 8 -> 0, of which waited for: 5 -> 0; matrix products, arithmetic and copies ran while one was open for 5% -> 0% of each run, Pallas kernels for 0% -> 0%
where the time goes in v1:
time: 153 us; the launch traced here: 152 us
  Pallas kernels  72.9 us (48%)
  local copies, waits for them, and re-layouts  36.3 us (24%)
  matrix products  31.7 us (21%)
  other arithmetic  9.64 us (6%)
  between operations  1.71 us (1%)
    pallas_call x1, Pallas kernels, reduce_density(): pl.pallas_call(functools.partial(reduce_kernel, pools, slabs), out_shape=...  47.1 us
    dot_general x4, matrix products, half_pass(): return jnp.einsum(spec, tables, values, preferred_element_type=jnp.float32)  28.4 us
    pallas_call x1, Pallas kernels, screened(): pl.pallas_call(functools.partial(screen_kernel, pools, slabs), out_shape=...  25.8 us
    dot_general x2, local copies, waits for them, and re-layouts, half_pass(): return jnp.einsum(spec, tables, values, preferred_element_type=jnp.float32)  15 us
    another operation x2, local copies, waits for them, and re-layouts  13.7 us
    mul x1, other arithmetic, weighted_intersection(): return jnp.sum(weights[:, None, None, None] * intersection, axis=0) * factor  7.76 us
    dot_general x4, matrix products, exact_pass(): jnp.einsum(spec, tables, values, precision=lax.Precision.HIGHEST, preferr...  3.23 us

profile of v1, /device:TPU:0, one launch (start us, length us, event | category | flops | bytes accessed | tf_op | source)
XLA Modules:
  0.0 152.2 jit_solution(14053115145300922320)
XLA Ops:
  0.0 0.2 multiply_convert_fusion
  0.2 0.2 multiply_convert_fusion.2
  0.5 7.9 %reshape.246 = bf16[2,96,96,96,1]{3,2,1,0,4:T(8,128)(2,1)} reshape(bf16[1,2,96,9216]{3,2,1,0:T(8,128)(2,1)} %param.12) | data formatting | bytes 7077888 | tf_op jit(solution)/shard_map/reshape.2
  8.4 6.9 %fusion.17 = bf16[2,96,96,96,1]{3,1,4,2,0:T(8,128)(2,1)} fusion(bf16[2,96,96,96,1]{3,2,1,0,4:T(8,128)(2,1)} %reshape.246, bf16[1,96,2,96]{3,1,2,0:T(8,128)(2,1)S(1)} %get-tuple-element.36, bf16[1,96,2,96]{3,1,2,0:T(8,128)(2,1)S(1)} %get-tuple-element.35), kind=kOutput, calls=%fused_computation.19 | convolution fusion | flops 679624704 | bytes 7151616 | tf_op jit(solution)/shard_map/rzsk,bskxy->brzxy/dot_general | solution.py:40
  15.3 7.5 %copy.30 = bf16[2,96,96,96,1]{2,3,0,1,4:T(8,128)(2,1)} copy(bf16[2,96,96,96,1]{3,1,4,2,0:T(8,128)(2,1)} %fusion.17) | data formatting | bytes 7077888 | tf_op jit(solution)/shard_map/rzsk,bskxy->brzxy/dot_general | solution.py:40
  22.8 7.6 %fusion.26 = f32[1,2,96,96,96]{4,3,1,2,0:T(8,128)} fusion(bf16[2,96,96,96,1]{2,3,0,1,4:T(8,128)(2,1)} %copy.30, bf16[1,96,2,96]{3,1,2,0:T(8,128)(2,1)} %copy-done.6, bf16[1,96,2,96]{3,1,2,0:T(8,128)(2,1)} %copy-done.4), kind=kOutput, calls=%fused_computation.22 | convolution fusion | flops 1361018880 | bytes 10690560 | tf_op jit(solution)/shard_map/rysk,bszxk->brzxy/dot_general | solution.py:40
  30.4 5.8 %reshape.252 = bf16[2,96,96,96,1]{3,2,1,0,4:T(8,128)(2,1)} reshape(bf16[1,2,96,9216]{3,2,1,0:T(8,128)(2,1)S(1)} %copy-done.3) | data formatting | bytes 7077888 | tf_op jit(solution)/shard_map/reshape.8
  36.1 7.0 %fusion.15 = bf16[2,96,96,96,1]{3,1,4,2,0:T(8,128)(2,1)} fusion(bf16[2,96,96,96,1]{3,2,1,0,4:T(8,128)(2,1)} %reshape.252, bf16[1,96,2,96]{3,1,2,0:T(8,128)(2,1)} %copy-done.6, bf16[1,96,2,96]{3,1,2,0:T(8,128)(2,1)} %copy-done.4), kind=kOutput, calls=%fused_computation.17 | convolution fusion | flops 679624704 | bytes 7151616 | tf_op jit(solution)/shard_map/rzsk,bskxy->brzxy/dot_general | solution.py:40
  43.1 7.5 %copy.36 = bf16[2,96,96,96,1]{2,3,0,1,4:T(8,128)(2,1)} copy(bf16[2,96,96,96,1]{3,1,4,2,0:T(8,128)(2,1)} %fusion.15) | data formatting | bytes 7077888 | tf_op jit(solution)/shard_map/rzsk,bskxy->brzxy/dot_general | solution.py:40
  50.7 7.0 %fusion.19 = f32[1,2,96,96,96]{4,3,1,2,0:T(8,128)} fusion(bf16[2,96,96,96,1]{2,3,0,1,4:T(8,128)(2,1)} %copy.36, bf16[1,96,2,96]{3,1,2,0:T(8,128)(2,1)S(1)} %copy-done.7, bf16[1,96,2,96]{3,1,2,0:T(8,128)(2,1)S(1)} %copy-done.5), kind=kOutput, calls=%fused_computation.21 | convolution fusion | flops 1361018880 | bytes 10690560 | tf_op jit(solution)/shard_map/rysk,bszxk->brzxy/dot_general | solution.py:40
  58.3 0.6 fusion.72
  59.6 7.8 %fusion.14 = f32[1,1,96,96,96]{4,3,1,2,0:T(8,128)S(1)} fusion(f32[1,2,96,96,96]{4,3,1,2,0:T(8,128)} %fusion.19, f32[1,2,96,96,96]{4,3,1,2,0:T(8,128)} %fusion.26, f32[]{:T(128)S(6)} %convert_element_type.82), kind=kLoop, calls=%fused_computation.15 | loop fusion | flops 4423680 | bytes 17694724 | tf_op jit(solution)/shard_map/mul | solution.py:51
  67.4 2.7 %copy.22 = f32[8,12,4,24,96]{4,3,1,2,0:T(8,128)} copy(f32[8,12,4,24,96]{4,3,2,1,0:T(8,128)S(1)} %bitcast.186) | data formatting | bytes 7077888 | tf_op jit(solution)/shard_map/mul | solution.py:51
  70.1 47.1 %shard_map.118 = f32[4,288,96]{2,1,0:T(8,128)} custom-call(f32[8,4,288,96]{3,2,1,0:T(8,128)} %bitcast.187), custom_call_target="tpu_custom_call" | custom-call | tf_op jit(solution)/shard_map/pallas_call | solution.py:175
  117.2 1.0 dynamic-slice_bitcast_fusion
  118.4 0.2 reshape.240
  119.1 0.6 convolution_bitcast_fusion
  119.7 0.7 constant_dynamic-slice_fusion.3
  120.6 0.7 convolution_bitcast_fusion.2
  121.9 25.8 %shard_map.119 = (f32[4,8,3,16,128]{4,3,2,1,0:T(8,128)S(1)}, f32[2,3,24,96]{3,2,1,0:T(8,128)S(1)}) custom-call(f32[8,3,16,128]{3,2,1,0:T(8,128)S(1)} %bitcast.184, f32[192,128]{1,0:T(8,128)S(1)} %copy-done.1, f32[256,96]{1,0:T(8,128)S(1)} %copy-done, f32[3,96,128]{2,1,0:T(8,128)S(1)} %compare_select_fusion.coulomb, f32[2,3,24,96]{3,2,1,0:T(8,128)S(1)} %pad_maximum_fusion.1.edges), custom_call_target="tpu_custom_call" | custom-call | tf_op jit(solution)/shard_map/pallas_call | solution.py:274
  147.8 1.5 %convolution_bitcast_fusion.1 = f32[2,12,24,128]{3,2,0,1:T(8,128)S(1)} fusion(f32[4,24,12,128]{3,2,1,0:T(8,128)S(1)} %bitcast.185, f32[4,2,24,4,24]{4,2,3,1,0:T(8,128)} %constant.93.clone, s32[]{:T(128)S(6)} %select_n.89), kind=kOutput, calls=%fused_computation.24 | convolution fusion | flops 84934656 | bytes 983044 | tf_op jit(solution)/shard_map/rxpk,pkzl->rzxl/dot_general | solution.py:34
  149.8 1.3 reshape.242
  151.1 0.3 convolution_add_fusion
  151.5 0.8 reshape.244
  (57 shorter events, 1.7 us)
Async XLA Ops:
  0.5 14.8 %copy-start.4 = (bf16[1,96,2,96]{3,1,2,0:T(8,128)(2,1)}, bf16[1,96,2,96]{3,1,2,0:T(8,128)(2,1)S(1)}, u32[]{:S(2)}) copy-start(bf16[1,96,2,96]{3,1,2,0:T(8,128)(2,1)S(1)} %get-tuple-element.35) | copy-start | bytes 110596
  0.5 14.8 %copy-start.6 = (bf16[1,96,2,96]{3,1,2,0:T(8,128)(2,1)}, bf16[1,96,2,96]{3,1,2,0:T(8,128)(2,1)S(1)}, u32[]{:S(2)}) copy-start(bf16[1,96,2,96]{3,1,2,0:T(8,128)(2,1)S(1)} %get-tuple-element.36) | copy-start | bytes 110596
  22.8 7.6 %copy-start.3 = (bf16[1,2,96,9216]{3,2,1,0:T(8,128)(2,1)S(1)}, bf16[1,2,96,9216]{3,2,1,0:T(8,128)(2,1)}, u32[]{:S(2)}) copy-start(bf16[1,2,96,9216]{3,2,1,0:T(8,128)(2,1)} %param.13) | copy-start | bytes 10616836
  43.1 7.5 %copy-start.5 = (bf16[1,96,2,96]{3,1,2,0:T(8,128)(2,1)S(1)}, bf16[1,96,2,96]{3,1,2,0:T(8,128)(2,1)}, u32[]{:S(2)}) copy-start(bf16[1,96,2,96]{3,1,2,0:T(8,128)(2,1)} %copy-done.4) | copy-start | bytes 110596
  43.1 7.5 %copy-start.7 = (bf16[1,96,2,96]{3,1,2,0:T(8,128)(2,1)S(1)}, bf16[1,96,2,96]{3,1,2,0:T(8,128)(2,1)}, u32[]{:S(2)}) copy-start(bf16[1,96,2,96]{3,1,2,0:T(8,128)(2,1)} %copy-done.6) | copy-start | bytes 110596
  50.7 7.6 %copy-start.11 = (s32[32]{0:T(128)S(1)}, s32[32]{0:T(128)}, u32[]{:S(2)}) copy-start(s32[32]{0:T(128)} %param.15) | copy-start | bytes 388
  70.1 48.3 %copy-start.8 = (f32[12,9216]{1,0:T(8,128)S(1)}, f32[12,9216]{1,0:T(8,128)}, u32[]{:S(2)}) copy-start(f32[12,9216]{1,0:T(8,128)} %param.17) | copy-start | bytes 1327108
  70.1 49.0 %copy-start.9 = (f32[96,128,1,1]{1,0,2,3:T(8,128)S(1)}, f32[96,128,1,1]{1,0,2,3:T(8,128)}, u32[]{:S(2)}) copy-start(f32[96,128,1,1]{1,0,2,3:T(8,128)} %constant.103) | copy-start | bytes 147460
  117.2 1.8 %copy-start.2 = (f32[4,288,96]{2,1,0:T(8,128)S(1)}, f32[4,288,96]{2,1,0:T(8,128)}, u32[]{:S(2)}) copy-start(f32[4,288,96]{2,1,0:T(8,128)} %shard_map.118) | copy-start | bytes 1327108
  118.3 3.6 %copy-start = (f32[256,96]{1,0:T(8,128)S(1)}, f32[256,96]{1,0:T(8,128)}, u32[]{:S(2)}) copy-start(f32[256,96]{1,0:T(8,128)} %constant.95.clone.back) | copy-start | bytes 294916
  118.3 3.6 %copy-start.1 = (f32[192,128]{1,0:T(8,128)S(1)}, f32[192,128]{1,0:T(8,128)}, u32[]{:S(2)}) copy-start(f32[192,128]{1,0:T(8,128)} %constant.94.clone.ahead) | copy-start | bytes 294916
  121.5 29.7 %copy-start.10 = (f32[128,96,1]{0,1,2:T(8,128)S(1)}, f32[128,96,1]{0,1,2:T(8,128)}, u32[]{:S(2)}) copy-start(f32[128,96,1]{0,1,2:T(8,128)} %constant.104) | copy-start | bytes 147460

commit v2 on v1

--- a/solution.py
+++ b/solution.py
@@ -36,39 +36,88 @@
     )
 
 
-def half_pass(spec, tables, values):
-    return jnp.einsum(spec, tables, values, preferred_element_type=jnp.float32)
-
-
 def band_weights(band_index, occupation):
     numbers = jnp.arange(occupation.shape[0], dtype=jnp.int32)
     matches = band_index[:, None] == numbers[None, :]
     return jnp.sum(jnp.where(matches, occupation[None, :], 0), axis=1).astype(jnp.float32)
 
 
-def weighted_intersection(wave_space, response_space, weights, factor):
-    intersection = wave_space[:, 0] * response_space[:, 0] + wave_space[:, 1] * response_space[:, 1]
-    return jnp.sum(weights[:, None, None, None] * intersection, axis=0) * factor
-
-
 def wrapped_window(block, first_row, width):
     extended = jnp.concatenate([block[:, -2:], block, block[:, :2]], axis=1)
     return lax.dynamic_slice_in_dim(extended, first_row, width + 4, 1)
 
 
+def band_kernel(bands, length, weight, wave, response, table, y_re, y_im, density, wave_cols, response_cols):
+    chunk = math.lcm(length, 128)
+    per = chunk // length
+    twice = 2 * length
+
+    def one_dot(a, b):
+        return jnp.dot(a, b, preferred_element_type=jnp.float32)
+
+    for b in range(bands):
+        for source, target in ((wave, wave_cols), (response, response_cols)):
+
+            def depth_step(c, carry, source=source, target=target):
+                start = pl.multiple_of(c * chunk, 128)
+                out = one_dot(table[...], source[b, :, pl.ds(start, chunk)])
+                for m in range(per):
+                    row = pl.multiple_of((c * per + m) * twice, 8)
+                    target[pl.ds(row, twice), 0:length] = out[:, m * length : (m + 1) * length]
+                return carry
+
+            lax.fori_loop(0, length * length // chunk, depth_step, 0, unroll=2)
+
+        def space(target, z):
+            pieces = []
+            for k in (0, 1):
+                halves = [
+                    target[pl.ds(z + k + s * length, length, stride=twice), :] for s in (0, 1)
+                ]
+                pieces.append(jnp.concatenate(halves, axis=0))
+            values = jnp.concatenate(pieces, axis=1).astype(jnp.bfloat16)
+            rows = one_dot(table[...], values).astype(jnp.bfloat16)
+            lanes = target.shape[1]
+            re, im = (
+                jnp.concatenate(
+                    [rows[r * length : (r + 1) * length, k * lanes : k * lanes + length] for k in (0, 1)],
+                    axis=0,
+                )
+                for r in (0, 1)
+            )
+            return one_dot(re, y_re[...]) + one_dot(im, y_im[...])
+
+        def plane_step(i, carry):
+            z = 2 * i
+            product = space(wave_cols, z) * space(response_cols, z)
+            half = product.shape[1] // 2
+            value = (product[:, :length] + product[:, half : half + length]) * weight[b]
+            for k in (0, 1):
+                part = value[k * length : (k + 1) * length]
+                density[z + k] = part if b == 0 else density[z + k] + part
+            return carry
+
+        lax.fori_loop(0, length // 2, plane_step, 0, unroll=2)
+
+
 def band_density(wave_coeff, response_coeff, weights, factor, slab_count, pool_count):
-    length = wave_coeff.shape[2]
-    cube_shape = (wave_coeff.shape[0], 2, length, length, length)
-    inverse_half = stacked_table(length, 1.0, jnp.bfloat16)
-
-    def to_space(coeff):
-        planes = half_pass("rzsk,bskxy->brzxy", inverse_half, coeff.reshape(cube_shape)).astype(
-            jnp.bfloat16
-        )
-        rows = half_pass("rxsk,bszky->brzxy", inverse_half, planes).astype(jnp.bfloat16)
-        return half_pass("rysk,bszxk->brzxy", inverse_half, rows)
-
-    density = weighted_intersection(to_space(wave_coeff), to_space(response_coeff), weights, factor)
+    bands, _, length, flat = wave_coeff.shape
+    shape = (bands, 2 * length, flat)
+    full = stacked_table(length, 1.0, jnp.bfloat16)
+    table = full.reshape(2 * length, 2 * length)
+    lanes = -(-length // 128) * 128
+    sides = ((0, 0), (0, lanes - length))
+    y_re = jnp.concatenate([jnp.pad(full[r, :, 0].T, sides) for r in (0, 1)], axis=1)
+    y_im = jnp.concatenate([jnp.pad(full[r, :, 1].T, sides) for r in (0, 1)], axis=1)
+    vmem = pl.BlockSpec(memory_space=pltpu.VMEM)
+    density = pl.pallas_call(
+        functools.partial(band_kernel, bands, length),
+        out_shape=jax.ShapeDtypeStruct((length, length, length), jnp.float32),
+        in_specs=[pl.BlockSpec(memory_space=pltpu.SMEM)] + [vmem] * 5,
+        out_specs=vmem,
+        scratch_shapes=[pltpu.VMEM((2 * length * length, lanes), jnp.float32)] * 2,
+        compiler_params=pltpu.CompilerParams(vmem_limit_bytes=48 * 2**20),
+    )(weights * factor, wave_coeff.reshape(shape), response_coeff.reshape(shape), table, y_re, y_im)
     density = density.reshape(
         slab_count, length // slab_count, pool_count, length // pool_count, length
     )

time: 153 us -> 131 us (0.86)
  Pallas kernels: 72.9 us -> 111 us
  matrix products: 31.7 us -> 3.23 us
  local copies, waits for them, and re-layouts: 36.3 us -> 12.2 us
  other arithmetic: 9.64 us -> 2.59 us
    pallas_call x0 -> x1, Pallas kernels: none -> 37.7 us  [band_density(): pl.pallas_call(functools.partial(band_kernel, bands, length), out_shape=j...]
    dot_general x4 -> x0, matrix products: 28.4 us -> none  [half_pass(): return jnp.einsum(spec, tables, values, preferred_element_type=jnp.float32)]
    dot_general x2 -> x0, local copies, waits for them, and re-layouts: 15 us -> none  [half_pass(): return jnp.einsum(spec, tables, values, preferred_element_type=jnp.float32)]
    another operation x2 -> x0, local copies, waits for them, and re-layouts: 13.7 us -> none
    mul x1 -> x2, other arithmetic: 7.76 us -> 0.44 us  [the longest x1 0.22 us: stacked_table(): cosine = jnp.cos(angles) * factor]
    reshape x0 -> x1, local copies, waits for them, and re-layouts: none -> 5.05 us  [band_density(): density.reshape(slab_count, length // slab_count, pool_count, length // p...]
    mul x1 -> x0, local copies, waits for them, and re-layouts: 2.72 us -> none  [weighted_intersection(): return jnp.sum(weights[:, None, None, None] * intersection, axis=0) * factor]
    unnamed x25 -> x15, local copies, waits for them, and re-layouts: 0.09 us -> 2.06 us
where the time goes in v2:
time: 131 us; the launch traced here: 130 us
  Pallas kernels  111 us (85%)
  local copies, waits for them, and re-layouts  12.2 us (9%)
  matrix products  3.23 us (2%)
  other arithmetic  2.59 us (2%)
  between operations  1.73 us (1%)
    pallas_call x1, Pallas kernels, reduce_density(): pl.pallas_call(functools.partial(reduce_kernel, pools, slabs), out_shape=...  47.1 us
    pallas_call x1, Pallas kernels, band_density(): pl.pallas_call(functools.partial(band_kernel, bands, length), out_shape=j...  37.7 us
    pallas_call x1, Pallas kernels, screened(): pl.pallas_call(functools.partial(screen_kernel, pools, slabs), out_shape=...  25.8 us
    reshape x1, local copies, waits for them, and re-layouts, band_density(): density.reshape(slab_count, length // slab_count, pool_count, length // p...  5.05 us
    dot_general x4, matrix products, exact_pass(): jnp.einsum(spec, tables, values, precision=lax.Precision.HIGHEST, preferr...  3.23 us

profile of v2, /device:TPU:0, one launch (start us, length us, event | category | flops | bytes accessed | tf_op | source)
XLA Modules:
  0.0 130.3 jit_solution(15566483875848161051)
XLA Ops:
  0.0 0.2 cosine_multiply_fusion
  0.2 0.2 fusion.36
  0.6 0.1 copy.18
  0.7 0.1 convert_element_type.66.table
  1.5 1.3 %fusion.41 = s32[]{:T(128)} fusion(s32[32]{0:T(128)} %param.15, s32[]{:T(128)} %bitcast.95), kind=kLoop, calls=%fused_computation.100 | loop fusion | flops 95 | bytes 136 | tf_op jit(solution)/shard_map/reduce_sum | solution.py:42
  3.4 2.0 %copy-done = bf16[1,2,96,9216]{3,2,1,0:T(8,128)(2,1)S(1)} copy-done((bf16[1,2,96,9216]{3,2,1,0:T(8,128)(2,1)S(1)}, bf16[1,2,96,9216]{3,2,1,0:T(8,128)(2,1)}, u32[]{:S(2)}) %copy-start) | copy-done | bytes 3538968
  5.4 37.7 %shard_map.118 = f32[96,96,96]{2,1,0:T(8,128)} custom-call(f32[1]{0:T(128)} %bitcast.2.weight, bf16[1,192,9216]{2,1,0:T(8,128)(2,1)S(1)} %bitcast.96, bf16[1,192,9216]{2,1,0:T(8,128)(2,1)} %bitcast.105, bf16[192,192]{1,0:T(8,128)(2,1)S(1)} %convert_element_type.66.table, bf16[96,256]{1,0:T(8,128)(2,1)S(1)} %fusion.30.y_re, bf16[96,256]{1,0:T(8,128)(2,1)S(1)} %fusion.31.y_im), custom_call_target="tpu_custom_call" | custom-call | tf_op jit(solution)/shard_map/pallas_call | solution.py:113
  43.1 5.1 %copy.19 = f32[8,12,4,24,96]{4,3,1,2,0:T(8,128)} copy(f32[8,12,4,24,96]{4,3,2,1,0:T(8,128)} %bitcast.99) | data formatting | bytes 7077888 | tf_op jit(solution)/shard_map/reshape | solution.py:121
  48.2 47.1 %shard_map.119 = f32[4,288,96]{2,1,0:T(8,128)} custom-call(f32[8,4,288,96]{3,2,1,0:T(8,128)} %bitcast.100), custom_call_target="tpu_custom_call" | custom-call | tf_op jit(solution)/shard_map/pallas_call | solution.py:224
  95.3 1.0 dynamic-slice_bitcast_fusion
  96.5 0.2 reshape.192
  96.7 0.2 fusion.19
  97.2 0.6 convolution_bitcast_fusion
  97.8 0.7 constant_dynamic-slice_fusion.3
  98.7 0.7 convolution_bitcast_fusion.2
  99.6 0.1 fusion.15
  99.8 0.1 compare_select_fusion.coulomb
  100.0 25.8 %shard_map.120 = (f32[4,8,3,16,128]{4,3,2,1,0:T(8,128)S(1)}, f32[2,3,24,96]{3,2,1,0:T(8,128)S(1)}) custom-call(f32[8,3,16,128]{3,2,1,0:T(8,128)S(1)} %bitcast.97, f32[192,128]{1,0:T(8,128)S(1)} %copy-done.2, f32[256,96]{1,0:T(8,128)S(1)} %copy-done.1, f32[3,96,128]{2,1,0:T(8,128)S(1)} %compare_select_fusion.coulomb, f32[2,3,24,96]{3,2,1,0:T(8,128)S(1)} %pad_maximum_fusion.edges), custom_call_target="tpu_custom_call" | custom-call | tf_op jit(solution)/shard_map/pallas_call | solution.py:323
  125.9 1.5 %convolution_bitcast_fusion.1 = f32[2,12,24,128]{3,2,0,1:T(8,128)S(1)} fusion(f32[4,24,12,128]{3,2,1,0:T(8,128)S(1)} %bitcast.98, f32[4,2,24,4,24]{4,2,3,1,0:T(8,128)} %constant.96.clone, s32[]{:T(128)S(6)} %select_n.89), kind=kOutput, calls=%fused_computation.1 | convolution fusion | flops 84934656 | bytes 983044 | tf_op jit(solution)/shard_map/rxpk,pkzl->rzxl/dot_general | solution.py:34
  127.6 0.1 fusion.2
  127.7 0.1 fusion.5
  127.9 1.3 reshape.194
  129.2 0.3 convolution_add_fusion
  129.5 0.8 reshape.196
  (45 shorter events, 1.1 us)
Async XLA Ops:
  3.4 2.0 %copy-start = (bf16[1,2,96,9216]{3,2,1,0:T(8,128)(2,1)S(1)}, bf16[1,2,96,9216]{3,2,1,0:T(8,128)(2,1)}, u32[]{:S(2)}) copy-start(bf16[1,2,96,9216]{3,2,1,0:T(8,128)(2,1)} %param.12) | copy-start | bytes 10616836
  48.1 48.3 %copy-start.4 = (f32[12,9216]{1,0:T(8,128)S(1)}, f32[12,9216]{1,0:T(8,128)}, u32[]{:S(2)}) copy-start(f32[12,9216]{1,0:T(8,128)} %param.17) | copy-start | bytes 1327108
  48.2 49.0 %copy-start.5 = (f32[96,128,1,1]{1,0,2,3:T(8,128)S(1)}, f32[96,128,1,1]{1,0,2,3:T(8,128)}, u32[]{:S(2)}) copy-start(f32[96,128,1,1]{1,0,2,3:T(8,128)} %constant.114) | copy-start | bytes 147460
  95.2 1.8 %copy-start.3 = (f32[4,288,96]{2,1,0:T(8,128)S(1)}, f32[4,288,96]{2,1,0:T(8,128)}, u32[]{:S(2)}) copy-start(f32[4,288,96]{2,1,0:T(8,128)} %shard_map.119) | copy-start | bytes 1327108
  96.3 3.6 %copy-start.1 = (f32[256,96]{1,0:T(8,128)S(1)}, f32[256,96]{1,0:T(8,128)}, u32[]{:S(2)}) copy-start(f32[256,96]{1,0:T(8,128)} %constant.98.clone.back) | copy-start | bytes 294916
  96.4 3.6 %copy-start.2 = (f32[192,128]{1,0:T(8,128)S(1)}, f32[192,128]{1,0:T(8,128)}, u32[]{:S(2)}) copy-start(f32[192,128]{1,0:T(8,128)} %constant.97.clone.ahead) | copy-start | bytes 294916
  99.5 29.6 %copy-start.6 = (f32[128,96,1]{0,1,2:T(8,128)S(1)}, f32[128,96,1]{0,1,2:T(8,128)}, u32[]{:S(2)}) copy-start(f32[128,96,1]{0,1,2:T(8,128)} %constant.115) | copy-start | bytes 147460
